TPU v7x, 32 devices: a whole 2x2x4 slice. The times are simulated.
32 devices in a mesh: lat: 8 (over z, x), depth: 4 (over y, core).
Axes of the slice: x: 2, y: 2, z: 4, core: 2. Of those that a mesh axis runs over, the one named last changes fastest.
Arguments:
- surface: float32 [128, 4096], P('lat'), may hold values from -6 to 6
- velocity: float32 [2, 128, 4096], P(None, 'lat'), may hold values from -6 to 6
- block_map: int32 [128, 4096], P('lat'), may hold values from 0 to 15
- free_flags: int32 [128, 4096], P('lat'), may hold values 0 or 1
- block_rates: float32 [16], replicated, may hold values from 0.2 to 2
- previous_mesh: float32 [128, 64, 4096], P('lat', 'depth'), may hold values from -6 to 6
Outputs:
- new_surface: float32 [128, 4096], P('lat')
- mesh_field: float32 [128, 64, 4096], P('lat', 'depth')
- column_norm: float32 [128], P('lat')
All inputs are finite; a program needn't handle non-finite values. No bound on the sum of `free_flags` on one device may be relied on, other than what follows from the above.
Results may differ from a plain program's by a relative error of at most 0.00002.
Values sent between devices are 32-bit elements; how exact they have to be, the bound alone decides.
A program may use at most 64 MiB of HBM per device.

v0:
```python
import jax
import jax.numpy as jnp
from jax import lax
from jax.sharding import PartitionSpec as P

ITERS = 2


TIME_STEP = 0.5
RELAX_WEIGHT = 0.8


def extended_2(block, sides, width):
    for axis, dim in sides:
        count = lax.axis_size(axis)
        forward = [(i, i + 1) for i in range(count - 1)]
        backward = [(target, source) for source, target in forward]
        low = lax.ppermute(
            lax.slice_in_dim(block, block.shape[dim] - width, None, axis=dim), axis, forward
        )
        high = lax.ppermute(lax.slice_in_dim(block, 0, width, axis=dim), axis, backward)
        block = jnp.concatenate([low, block, high], axis=dim)
    return block


def advect(surface, velocity, block_map, free_flags, block_rates):
    widened = jnp.pad(surface, ((0, 0), (1, 1)))
    extended = extended_2(widened, (("lat", 0),), 1)
    middle = extended[1:-1, 1:-1]
    grad_rows = (extended[2:, 1:-1] - extended[:-2, 1:-1]) * 0.5
    grad_cols = (extended[1:-1, 2:] - extended[1:-1, :-2]) * 0.5
    laplace = (
        extended[2:, 1:-1]
        + extended[:-2, 1:-1]
        + extended[1:-1, 2:]
        + extended[1:-1, :-2]
        - 4.0 * middle
    )
    labels = jnp.arange(block_rates.shape[0], dtype=jnp.int32)
    matches = block_map[None, :, :] == labels[:, None, None]
    diffusivity = jnp.sum(jnp.where(matches, block_rates[:, None, None], 0.0), axis=0)
    velocity_rows = velocity[0]
    velocity_cols = velocity[1]
    tendency = -velocity_rows * grad_rows - velocity_cols * grad_cols + diffusivity * laplace
    return middle + TIME_STEP * free_flags.astype(jnp.float32) * tendency


def relax_core(extended):
    current = extended[1:-1, 1:-1]
    across_rows = extended[2:, 1:-1] + extended[:-2, 1:-1]
    padded_cols = jnp.pad(current, ((0, 0), (0, 0), (1, 1)))
    across_cols = padded_cols[:, :, 2:] + padded_cols[:, :, :-2]
    upper = extended[1:-1, :-2]
    lower = extended[1:-1, 2:]
    neighbours = across_rows + across_cols + upper + lower
    return (current, (1.0 - RELAX_WEIGHT) * current + RELAX_WEIGHT * neighbours / 6.0)


def deep_sweeps(extended, shift_rim, rows_here, layers_here, total_rows, total_layers, at_top):
    global_rows = (
        lax.axis_index("lat") * rows_here
        - ITERS
        + jnp.arange(rows_here + 2 * ITERS, dtype=jnp.int32)
    )
    global_layers = (
        lax.axis_index("depth") * layers_here
        - ITERS
        + jnp.arange(layers_here + 2 * ITERS, dtype=jnp.int32)
    )
    ghost = jnp.where(at_top, shift_rim, extended[:, ITERS - 1, :])
    extended = extended.at[:, ITERS - 1, :].set(ghost)
    for sweep_index in range(ITERS):
        rows_now = global_rows[sweep_index + 1 : global_rows.shape[0] - sweep_index - 1]
        layers_now = global_layers[sweep_index + 1 : global_layers.shape[0] - sweep_index - 1]
        inside_rows = (rows_now >= 0) & (rows_now < total_rows)
        inside_layers = (layers_now >= 0) & (layers_now < total_layers)
        inside = inside_rows[:, None, None] & inside_layers[None, :, None]
        current, updated = relax_core(extended)
        extended = jnp.where(inside, updated, current)
    return extended


def per_device(surface, velocity, block_map, free_flags, block_rates, previous_mesh):
    columns = surface.shape[1]
    new_surface = advect(surface, velocity, block_map, free_flags, block_rates)
    surface_shift = new_surface - surface
    rows_here = previous_mesh.shape[0]
    layers_here = previous_mesh.shape[1]
    total_rows = rows_here * lax.axis_size("lat")
    total_layers = layers_here * lax.axis_size("depth")
    at_top = lax.axis_index("depth") == 0
    layers = lax.axis_index("depth") * layers_here + jnp.arange(layers_here, dtype=jnp.int32)
    profile = (total_layers - layers).astype(jnp.float32) / total_layers
    field = previous_mesh + surface_shift[:, None, :] * profile[None, :, None]
    shift_rim = extended_2(surface_shift, (("lat", 0),), ITERS)
    extended = extended_2(field, (("lat", 0), ("depth", 1)), ITERS)
    field = deep_sweeps(
        extended, shift_rim, rows_here, layers_here, total_rows, total_layers, at_top
    )
    local_sums = jnp.sum(field * field, axis=(1, 2))
    total_sums = lax.psum(local_sums, "depth")
    column_norm = jnp.sqrt(total_sums / (total_layers * columns))
    return (new_surface, field, column_norm)


def solution(mesh):
    in_specs = (
        P("lat", None),
        P(None, "lat", None),
        P("lat", None),
        P("lat", None),
        P(),
        P("lat", "depth", None),
    )
    out_specs = (P("lat", None), P("lat", "depth", None), P("lat"))
    return jax.shard_map(
        per_device, mesh=mesh, in_specs=in_specs, out_specs=out_specs, check_vma=False
    )
```

profile of v0, /device:TPU:11, one launch (start us, length us, event | category | flops | bytes accessed | tf_op | source)
XLA Modules:
  0.0 110.6 jit_solution(15345543036470811492)
XLA Ops:
  0.6 1.1 pad_slice_fusion.1
  1.7 3.2 %collective-permute-start.1 = (f32[1,4098]{1,0:T(1,128)S(1)}, f32[1,4098]{1,0:T(1,128)S(1)}, u32[]{:S(2)}, u32[]{:S(2)}) collective-permute-start(f32[1,4098]{1,0:T(1,128)S(1)} %get-tuple-element.29), channel_id=1, source_target_pairs={{0,4},{4,8},{8,12},{12,16},{16,20},{20,24},{24,28},{1,5},{5,9},{9,... | collective-permute-start | bytes 49184 | tf_op jit(solution)/shard_map/ppermute | solution.py:18
  4.9 2.1 %collective-permute-start = (f32[1,4098]{1,0:T(1,128)S(1)}, f32[1,4098]{1,0:T(1,128)S(1)}, u32[]{:S(2)}, u32[]{:S(2)}) collective-permute-start(f32[1,4098]{1,0:T(1,128)S(1)} %get-tuple-element.28), channel_id=1, source_target_pairs={{4,0},{8,4},{12,8},{16,12},{20,16},{24,20},{28,24},{5,1},{9,5},{13... | collective-permute-start | bytes 49184 | tf_op jit(solution)/shard_map/ppermute | solution.py:21
  7.1 1.5 %select_reduce_fusion = f32[16,4096]{1,0:T(8,128)S(1)} fusion(f32[16]{0:T(128)} %param.12, s32[16,4096]{1,0:T(8,128)} %param.10), kind=kLoop, calls=%fused_computation.17 | loop fusion | flops 3080192 | bytes 524352 | tf_op jit(solution)/shard_map/reduce_sum | solution.py:41
  8.6 1.1 pad.14
  10.3 2.2 %fusion.13 = (f32[16,4096]{1,0:T(8,128)S(1)}, f32[16,4096]{1,0:T(8,128)}) fusion(f32[16,4096]{1,0:T(8,128)} %param.8, f32[16,4096]{1,0:T(8,128)S(1)} %select_reduce_fusion, f32[16,4098]{1,0:T(8,128)S(1)} %pad.14, f32[2,16,4096]{2,1,0:T(8,128)} %param.9, f32[1,4098]{1,0:T(1,128)S(1)} %collective-permute-done.1, f32[1,4098]{1,0:T(1,128)S(1)} %collective-permute-done, ...), kind=kLoop, calls=%fused_computation.43 | loop fusion | flops 1441792 | bytes 2663424 | tf_op jit(solution)/shard_map/sub | solution.py:86
  12.6 2.8 %multiply_add_fusion = f32[16,16,4096]{2,1,0:T(8,128)S(1)} fusion(f32[16,16,4096]{2,1,0:T(8,128)} %param.13, f32[16]{0:T(128)S(1)} %convert_multiply_fusion, f32[16,4096]{1,0:T(8,128)S(1)} %get-tuple-element.20), kind=kLoop, calls=%fused_computation.16 | loop fusion | flops 2097152 | bytes 8650816 | tf_op jit(solution)/shard_map/add | solution.py:94
  15.5 2.4 %collective-permute-start.3 = (f32[2,16,4096]{2,1,0:T(8,128)S(1)}, f32[2,16,4096]{2,1,0:T(8,128)S(1)}, u32[]{:S(2)}, u32[]{:S(2)}) collective-permute-start(f32[2,16,4096]{2,1,0:T(8,128)S(1)} %get-tuple-element.25), channel_id=1, source_target_pairs={{4,0},{8,4},{12,8},{16,12},{20,16},{24,20},{28,24},{5,1},{9,5},{13... | collective-permute-start | bytes 1572872 | tf_op jit(solution)/shard_map/ppermute | solution.py:21
  17.9 3.8 %collective-permute-start.2 = (f32[2,16,4096]{2,1,0:T(8,128)S(1)}, f32[2,16,4096]{2,1,0:T(8,128)S(1)}, u32[]{:S(2)}, u32[]{:S(2)}) collective-permute-start(f32[2,16,4096]{2,1,0:T(8,128)S(1)} %get-tuple-element.24), channel_id=1, source_target_pairs={{0,4},{4,8},{8,12},{12,16},{16,20},{20,24},{24,28},{1,5},{5,9},{9,... | collective-permute-start | bytes 1572872 | tf_op jit(solution)/shard_map/ppermute | solution.py:18
  21.9 17.2 %collective-permute-done.3 = f32[2,16,4096]{2,1,0:T(8,128)S(1)} collective-permute-done((f32[2,16,4096]{2,1,0:T(8,128)S(1)}, f32[2,16,4096]{2,1,0:T(8,128)S(1)}, u32[]{:S(2)}, u32[]{:S(2)}) %collective-permute-start.3) | collective-permute-done | bytes 524320 | tf_op jit(solution)/shard_map/ppermute | solution.py:21
  39.1 4.3 %collective-permute-done.2 = f32[2,16,4096]{2,1,0:T(8,128)S(1)} collective-permute-done((f32[2,16,4096]{2,1,0:T(8,128)S(1)}, f32[2,16,4096]{2,1,0:T(8,128)S(1)}, u32[]{:S(2)}, u32[]{:S(2)}) %collective-permute-start.2) | collective-permute-done | bytes 524320 | tf_op jit(solution)/shard_map/ppermute | solution.py:18
  43.3 1.4 %pad_maximum_fusion.3 = (f32[20,2,4096]{2,1,0:T(2,128)}, f32[20,2,4096]{2,1,0:T(2,128)S(1)}) fusion(f32[2,16,4096]{2,1,0:T(8,128)S(1)} %collective-permute-done.3, f32[16,16,4096]{2,1,0:T(8,128)S(1)} %multiply_add_fusion, f32[2,16,4096]{2,1,0:T(8,128)S(1)} %collective-permute-done.2), kind=kLoop, calls=%fused_computation.21 | loop fusion | flops 655360 | bytes 6553600 | tf_op jit(solution)/shard_map/slice | solution.py:19
  44.7 3.5 %collective-permute-start.4 = (f32[20,2,4096]{2,1,0:T(2,128)}, f32[20,2,4096]{2,1,0:T(2,128)S(1)}, u32[]{:S(2)}, u32[]{:S(2)}) collective-permute-start(f32[20,2,4096]{2,1,0:T(2,128)} %get-tuple-element.22), channel_id=1, source_target_pairs={{0,1},{1,2},{2,3},{4,5},{5,6},{6,7},{8,9},{9,10},{10,11},{12,13},{... | collective-permute-start | bytes 1966088 | tf_op jit(solution)/shard_map/ppermute | solution.py:18
  48.3 1.9 %collective-permute-start.7 = (f32[2,4096]{1,0:T(2,128)S(1)}, f32[2,4096]{1,0:T(2,128)S(1)}, u32[]{:S(2)}, u32[]{:S(2)}) collective-permute-start(f32[2,4096]{1,0:T(2,128)S(1)} %get-tuple-element.27), channel_id=1, source_target_pairs={{4,0},{8,4},{12,8},{16,12},{20,16},{24,20},{28,24},{5,1},{9,5},{13... | collective-permute-start | bytes 98312 | tf_op jit(solution)/shard_map/ppermute | solution.py:21
  50.2 4.3 %collective-permute-start.6 = (f32[2,4096]{1,0:T(2,128)S(1)}, f32[2,4096]{1,0:T(2,128)S(1)}, u32[]{:S(2)}, u32[]{:S(2)}) collective-permute-start(f32[2,4096]{1,0:T(2,128)S(1)} %get-tuple-element.26), channel_id=1, source_target_pairs={{0,4},{4,8},{8,12},{12,16},{16,20},{20,24},{24,28},{1,5},{5,9},{9,... | collective-permute-start | bytes 98312 | tf_op jit(solution)/shard_map/ppermute | solution.py:18
  54.5 1.9 %collective-permute-start.5 = (f32[20,2,4096]{2,1,0:T(2,128)S(1)}, f32[20,2,4096]{2,1,0:T(2,128)S(1)}, u32[]{:S(2)}, u32[]{:S(2)}) collective-permute-start(f32[20,2,4096]{2,1,0:T(2,128)S(1)} %get-tuple-element.23), channel_id=1, source_target_pairs={{1,0},{2,1},{3,2},{5,4},{6,5},{7,6},{9,8},{10,9},{11,10},{13,12},{... | collective-permute-start | bytes 1966088 | tf_op jit(solution)/shard_map/ppermute | solution.py:21
  57.4 9.0 %collective-permute-done.5 = f32[20,2,4096]{2,1,0:T(2,128)S(1)} collective-permute-done((f32[20,2,4096]{2,1,0:T(2,128)S(1)}, f32[20,2,4096]{2,1,0:T(2,128)S(1)}, u32[]{:S(2)}, u32[]{:S(2)}) %collective-permute-start.5) | collective-permute-done | bytes 655392 | tf_op jit(solution)/shard_map/ppermute | solution.py:21
  66.4 5.5 %pad_maximum_fusion = f32[20,20,4096]{2,1,0:T(8,128)} fusion(f32[20,2,4096]{2,1,0:T(2,128)S(1)} %collective-permute-done.5, f32[2,16,4096]{2,1,0:T(8,128)S(1)} %collective-permute-done.3, f32[16,16,4096]{2,1,0:T(8,128)} %copy-done.1, f32[2,16,4096]{2,1,0:T(8,128)S(1)} %collective-permute-done.2, f32[20,2,4096]{2,1,0:T(2,128)S(1)} %collective-permute-done.4), kind=kLoop, calls=%fused_computation | loop fusion | flops 6553600 | bytes 13107200 | tf_op jit(solution)/shard_map/concatenate | solution.py:22
  71.9 7.2 %scatter.4 = f32[20,20,4096]{2,1,0:T(8,128)} dynamic-update-slice(f32[20,20,4096]{2,1,0:T(8,128)} %pad_maximum_fusion, f32[20,1,4096]{2,1,0:T(1,128)S(1)} %copy.18, s32[]{:T(128)} %constant.69.clone.1, s32[]{:T(128)} %constant.74.clone.1, s32[]{:T(128)} %constant.69.clone.1) | dynamic-update-slice | bytes 655364 | tf_op jit(solution)/shard_map/scatter | solution.py:71
  79.1 7.5 %slice.164 = f32[18,18,4096]{2,1,0:T(8,128)} slice(f32[20,20,4096]{2,1,0:T(8,128)} %scatter.4), slice={[1:19], [1:19], [0:4096]} | slice | bytes 10616832 | tf_op jit(solution)/shard_map/slice | solution.py:49
  86.5 12.7 %fusion.2 = f32[18,18,4096]{2,1,0:T(8,128)S(1)} fusion(f32[18,18,4096]{2,1,0:T(8,128)} %slice.164, f32[20,20,4096]{2,1,0:T(8,128)S(1)} %copy-done, pred[18,18]{1,0:T(8,128)(4,1)S(1)} %broadcast_and_fusion), kind=kLoop, calls=%fused_computation.4 | loop fusion | flops 11943936 | bytes 31850820 | tf_op jit(solution)/shard_map/jit(_where)/select_n | solution.py:79
  99.2 0.7 slice.169
  99.9 5.1 %multiply_reduce_fusion = (f32[16]{0:T(128)S(1)}, f32[16,16,4096]{2,1,0:T(8,128)}) fusion(f32[16,16,4096]{2,1,0:T(8,128)S(1)} %slice.169, f32[18,18,4096]{2,1,0:T(8,128)S(1)} %fusion.2, pred[16,16]{1,0:T(8,128)(4,1)S(1)} %broadcast_and_fusion.1), kind=kLoop, calls=%fused_computation.15 | loop fusion | flops 11534320 | bytes 25166144 | tf_op jit(solution)/shard_map/reduce_sum | solution.py:100
  105.0 5.1 %psum.7 = f32[16]{0:T(128)S(1)} all-reduce(f32[16]{0:T(128)S(1)} %get-tuple-element.18), channel_id=1, replica_groups=mesh['lat'=8,'depth'=4] {'depth'}, use_global_device_ids=true, to_apply=%region_2.3 | all-reduce | flops 16 | bytes 128 | tf_op jit(solution)/shard_map/psum | solution.py:101
  (22 shorter events, 2.5 us)
Async XLA Ops:
  1.7 7.9 %collective-permute-start.1 = (f32[1,4098]{1,0:T(1,128)S(1)}, f32[1,4098]{1,0:T(1,128)S(1)}, u32[]{:S(2)}, u32[]{:S(2)}) collective-permute-start(f32[1,4098]{1,0:T(1,128)S(1)} %get-tuple-element.29), channel_id=1, source_target_pairs={{0,4},{4,8},{8,12},{12,16},{16,20},{20,24},{24,28},{1,5},{5,9},{9,... | collective-permute-start | bytes 49184 | tf_op jit(solution)/shard_map/ppermute | solution.py:18
  4.9 5.4 %collective-permute-start = (f32[1,4098]{1,0:T(1,128)S(1)}, f32[1,4098]{1,0:T(1,128)S(1)}, u32[]{:S(2)}, u32[]{:S(2)}) collective-permute-start(f32[1,4098]{1,0:T(1,128)S(1)} %get-tuple-element.28), channel_id=1, source_target_pairs={{4,0},{8,4},{12,8},{16,12},{20,16},{24,20},{28,24},{5,1},{9,5},{13... | collective-permute-start | bytes 49184 | tf_op jit(solution)/shard_map/ppermute | solution.py:21
  15.4 29.3 %copy-start.1 = (f32[16,16,4096]{2,1,0:T(8,128)}, f32[16,16,4096]{2,1,0:T(8,128)S(1)}, u32[]{:S(2)}) copy-start(f32[16,16,4096]{2,1,0:T(8,128)S(1)} %multiply_add_fusion) | copy-start | bytes 12582916
  15.5 23.6 %collective-permute-start.3 = (f32[2,16,4096]{2,1,0:T(8,128)S(1)}, f32[2,16,4096]{2,1,0:T(8,128)S(1)}, u32[]{:S(2)}, u32[]{:S(2)}) collective-permute-start(f32[2,16,4096]{2,1,0:T(8,128)S(1)} %get-tuple-element.25), channel_id=1, source_target_pairs={{4,0},{8,4},{12,8},{16,12},{20,16},{24,20},{28,24},{5,1},{9,5},{13... | collective-permute-start | bytes 1572872 | tf_op jit(solution)/shard_map/ppermute | solution.py:21
  17.9 25.4 %collective-permute-start.2 = (f32[2,16,4096]{2,1,0:T(8,128)S(1)}, f32[2,16,4096]{2,1,0:T(8,128)S(1)}, u32[]{:S(2)}, u32[]{:S(2)}) collective-permute-start(f32[2,16,4096]{2,1,0:T(8,128)S(1)} %get-tuple-element.24), channel_id=1, source_target_pairs={{0,4},{4,8},{8,12},{12,16},{16,20},{20,24},{24,28},{1,5},{5,9},{9,... | collective-permute-start | bytes 1572872 | tf_op jit(solution)/shard_map/ppermute | solution.py:18
  44.7 11.8 %collective-permute-start.4 = (f32[20,2,4096]{2,1,0:T(2,128)}, f32[20,2,4096]{2,1,0:T(2,128)S(1)}, u32[]{:S(2)}, u32[]{:S(2)}) collective-permute-start(f32[20,2,4096]{2,1,0:T(2,128)} %get-tuple-element.22), channel_id=1, source_target_pairs={{0,1},{1,2},{2,3},{4,5},{5,6},{6,7},{8,9},{9,10},{10,11},{12,13},{... | collective-permute-start | bytes 1966088 | tf_op jit(solution)/shard_map/ppermute | solution.py:18
  48.3 8.6 %collective-permute-start.7 = (f32[2,4096]{1,0:T(2,128)S(1)}, f32[2,4096]{1,0:T(2,128)S(1)}, u32[]{:S(2)}, u32[]{:S(2)}) collective-permute-start(f32[2,4096]{1,0:T(2,128)S(1)} %get-tuple-element.27), channel_id=1, source_target_pairs={{4,0},{8,4},{12,8},{16,12},{20,16},{24,20},{28,24},{5,1},{9,5},{13... | collective-permute-start | bytes 98312 | tf_op jit(solution)/shard_map/ppermute | solution.py:21
  50.2 6.6 %collective-permute-start.6 = (f32[2,4096]{1,0:T(2,128)S(1)}, f32[2,4096]{1,0:T(2,128)S(1)}, u32[]{:S(2)}, u32[]{:S(2)}) collective-permute-start(f32[2,4096]{1,0:T(2,128)S(1)} %get-tuple-element.26), channel_id=1, source_target_pairs={{0,4},{4,8},{8,12},{12,16},{16,20},{20,24},{24,28},{1,5},{5,9},{9,... | collective-permute-start | bytes 98312 | tf_op jit(solution)/shard_map/ppermute | solution.py:18
  54.5 11.9 %collective-permute-start.5 = (f32[20,2,4096]{2,1,0:T(2,128)S(1)}, f32[20,2,4096]{2,1,0:T(2,128)S(1)}, u32[]{:S(2)}, u32[]{:S(2)}) collective-permute-start(f32[20,2,4096]{2,1,0:T(2,128)S(1)} %get-tuple-element.23), channel_id=1, source_target_pairs={{1,0},{2,1},{3,2},{5,4},{6,5},{7,6},{9,8},{10,9},{11,10},{13,12},{... | collective-permute-start | bytes 1966088 | tf_op jit(solution)/shard_map/ppermute | solution.py:21
  79.1 7.5 %copy-start = (f32[20,20,4096]{2,1,0:T(8,128)S(1)}, f32[20,20,4096]{2,1,0:T(8,128)}, u32[]{:S(2)}) copy-start(f32[20,20,4096]{2,1,0:T(8,128)} %scatter.4) | copy-start | bytes 19660804
where the time goes:
time: 112 us; the launch traced here: 111 us
  other arithmetic  32.2 us (29%)
  waiting for transfers between devices  31.1 us (28%)
  starting transfers between devices  23.1 us (21%)
  local copies, waits for them, and re-layouts  18.3 us (16%)
  blocking collectives  5.09 us (5%)
    ppermute x4, waiting for transfers between devices, extended_2(): lax.ppermute(lax.slice_in_dim(block, 0, width, axis=dim), axis, backward)  26.8 us
    ppermute x4, starting transfers between devices, extended_2(): lax.ppermute(lax.slice_in_dim(block, block.shape[dim] - width, None, axis...  14.7 us
    select_n x1, other arithmetic, deep_sweeps(): extended = jnp.where(inside, updated, current)  12.7 us
    ppermute x4, starting transfers between devices, extended_2(): lax.ppermute(lax.slice_in_dim(block, 0, width, axis=dim), axis, backward)  8.36 us
    slice x2, local copies, waits for them, and re-layouts, relax_core(): current = extended[1:-1, 1:-1]  8.14 us
    scatter x1, local copies, waits for them, and re-layouts, deep_sweeps(): extended = extended.at[:, ITERS - 1, :].set(ghost)  7.18 us
    concatenate x1, other arithmetic, extended_2(): block = jnp.concatenate([low, block, high], axis=dim)  5.46 us
    reduce_sum x1, other arithmetic, per_device(): local_sums = jnp.sum(field * field, axis=(1, 2))  5.12 us
  transfers between devices with their start and end apart: 8, of which 4 were waited for; matrix products, arithmetic and copies ran while one was open for 3% of the time, Pallas kernels for 0%

commit v1 on v0

v1 whole, which is shorter than its diff:
```python
import functools

import jax
import jax.numpy as jnp
from jax import lax
from jax.experimental import pallas as pl
from jax.experimental.pallas import tpu as pltpu
from jax.sharding import PartitionSpec as P

ITERS = 2
TIME_STEP = 0.5
RELAX_WEIGHT = 0.8
MESH = pl.DeviceIdType.MESH
PAD = 128
TILE = 8
WIDTH = 512
CHUNKS = 4
EARLY = 3
SURF, SHIFT, FIRST = 0, 1, 2


def lanes_beside(window, width):
    span = window.shape[1]
    left = pltpu.roll(window, 1, 1)[:, PAD : PAD + width]
    right = pltpu.roll(window, span - 1, 1)[:, PAD : PAD + width]
    return window[:, PAD : PAD + width], left, right


def kernel(
    lats,
    depths,
    surface,
    velocity,
    block_map,
    free_flags,
    rates,
    previous,
    new_surface,
    field,
    norm,
    surf,
    vel,
    blocks,
    flags,
    shift,
    moved,
    first,
    second,
    result,
    squares,
    sums,
    others,
    local_sem,
    out_sem,
    lat_send,
    lat_recv,
    depth_send,
    depth_recv,
    sum_send,
    sum_recv,
):
    rows, layers, columns = previous.shape
    lat = lax.axis_index("lat")
    depth = lax.axis_index("depth")
    total_layers = layers * depths
    blocks_count = rates.shape[0]
    steps = columns // WIDTH
    piece = columns // CHUNKS
    has_low, has_high = lat > 0, lat < lats - 1
    has_above, has_below = depth > 0, depth < depths - 1
    body_rows = pl.ds(TILE, rows)
    body_layers = pl.ds(TILE, layers)
    body_cols = pl.ds(PAD, columns)

    locals_ = [
        pltpu.make_async_copy(surface, surf.at[body_rows, body_cols], local_sem.at[0]),
        pltpu.make_async_copy(velocity, vel, local_sem.at[1]),
        pltpu.make_async_copy(block_map, blocks, local_sem.at[2]),
        pltpu.make_async_copy(free_flags, flags, local_sem.at[3]),
        pltpu.make_async_copy(
            previous, first.at[pl.ds(1, rows), body_layers, body_cols], local_sem.at[4]
        ),
    ]
    for copy in locals_:
        copy.start()

    barrier = pltpu.get_barrier_semaphore()

    def greet(target):
        pl.semaphore_signal(barrier, inc=1, device_id=target, device_id_type=MESH)

    low_id = {"lat": jnp.maximum(lat - 1, 0)}
    high_id = {"lat": jnp.minimum(lat + 1, lats - 1)}
    above_id = {"depth": jnp.maximum(depth - 1, 0)}
    below_id = {"depth": jnp.minimum(depth + 1, depths - 1)}

    pl.when(has_low)(lambda: greet(low_id))
    pl.when(has_high)(lambda: greet(high_id))
    for k in range(1, depths):
        greet({"depth": lax.rem(depth + k, depths)})
    peers = depths - 1 + has_low.astype(jnp.int32) + has_high.astype(jnp.int32)
    pl.semaphore_wait(barrier, peers)

    def lateral(side, slot, src, dst):
        return pltpu.make_async_remote_copy(
            src_ref=src,
            dst_ref=dst,
            send_sem=lat_send.at[side, slot],
            recv_sem=lat_recv.at[side, slot],
            device_id=high_id if side == 0 else low_id,
            device_id_type=MESH,
        )

    def vertical(side, slot, src, dst):
        return pltpu.make_async_remote_copy(
            src_ref=src,
            dst_ref=dst,
            send_sem=depth_send.at[side, slot],
            recv_sem=depth_recv.at[side, slot],
            device_id=below_id if side == 0 else above_id,
            device_id_type=MESH,
        )

    def piece_cols(k):
        return pl.ds(PAD + k * piece, piece)

    lat_sends = (has_high, has_low)
    lat_recvs = (has_low, has_high)
    depth_sends = (has_below, has_above)
    depth_recvs = (has_above, has_below)
    own_edge = (rows, 1)
    far_edge = (0, rows + 1)
    own_layer = (TILE + layers - 1, TILE)
    far_layer = (TILE - 1, TILE + layers)

    surf_copies = [
        lateral(
            side,
            SURF,
            surface.at[pl.ds((rows - 1, 0)[side], 1), :],
            surf.at[pl.ds((TILE - 1, TILE + rows)[side], 1), body_cols],
        )
        for side in (0, 1)
    ]
    shift_copies = [
        lateral(
            side,
            SHIFT,
            shift.at[pl.ds((TILE + rows - 1, TILE)[side], 1), :],
            shift.at[pl.ds((TILE - 1, TILE + rows)[side], 1), :],
        )
        for side in (0, 1)
    ]
    first_copies = [
        [
            lateral(
                side,
                FIRST + k,
                previous.at[(rows - 1, 0)[side], :, pl.ds(k * piece, piece)],
                first.at[far_edge[side], body_layers, piece_cols(k)],
            )
            for side in (0, 1)
        ]
        for k in range(CHUNKS)
    ]
    second_copies = [
        [
            lateral(
                side,
                FIRST + CHUNKS + k,
                second.at[own_edge[side], body_layers, piece_cols(k)],
                second.at[far_edge[side], body_layers, piece_cols(k)],
            )
            for side in (0, 1)
        ]
        for k in range(CHUNKS)
    ]
    layer_copies = [
        vertical(
            side,
            0,
            previous.at[:, pl.ds((layers - 1, 0)[side], 1), :],
            first.at[pl.ds(1, rows), pl.ds(far_layer[side], 1), body_cols],
        )
        for side in (0, 1)
    ]
    spans = (pl.ds(2, rows - 2), pl.ds(1, 1), pl.ds(rows, 1))
    later_layers = [
        [
            vertical(
                side,
                1 + j,
                second.at[span, pl.ds(own_layer[side], 1), body_cols],
                second.at[span, pl.ds(far_layer[side], 1), body_cols],
            )
            for side in (0, 1)
        ]
        for j, span in enumerate(spans)
    ]
    sum_copies = [
        pltpu.make_async_remote_copy(
            src_ref=sums,
            dst_ref=others.at[k - 1],
            send_sem=sum_send.at[k - 1],
            recv_sem=sum_recv.at[k - 1],
            device_id={"depth": lax.rem(depth + k, depths)},
            device_id_type=MESH,
        )
        for k in range(1, depths)
    ]

    for side in (0, 1):
        pl.when(lat_sends[side])(surf_copies[side].start)
    for side in (0, 1):
        pl.when(depth_sends[side])(layer_copies[side].start)
    for k in range(EARLY):
        for side in (0, 1):
            pl.when(lat_sends[side])(first_copies[k][side].start)

    zero_tile = jnp.zeros((layers, PAD), jnp.float32)

    def clear_pads(r, carry):
        for buffer in (first, second):
            for start in (0, PAD + columns):
                buffer[r, body_layers, pl.ds(start, PAD)] = zero_tile
        return carry

    lax.fori_loop(1, rows + 1, clear_pads, 0)
    for start in (0, PAD + columns):
        surf[body_rows, pl.ds(start, PAD)] = jnp.zeros((rows, PAD), jnp.float32)
    squares[...] = jnp.zeros_like(squares)

    for side in (0, 1):

        @pl.when(jnp.logical_not(lat_recvs[side]))
        def _(side=side):
            surf[pl.ds((TILE - 1, TILE + rows)[side], 1), body_cols] = jnp.zeros(
                (1, columns), jnp.float32
            )
            shift[pl.ds((TILE - 1, TILE + rows)[side], 1), :] = jnp.zeros(
                (1, columns), jnp.float32
            )
            for buffer in (first, second):
                buffer[far_edge[side], body_layers, body_cols] = jnp.zeros(
                    (layers, columns), jnp.float32
                )

    for copy in locals_[:4]:
        copy.wait()
    for side in (0, 1):
        pl.when(lat_recvs[side])(surf_copies[side].wait_recv)

    def advect(step, carry):
        c = pl.multiple_of(step * WIDTH, WIDTH)
        cols = pl.ds(c, WIDTH)
        inner = pl.ds(pl.multiple_of(c + PAD, PAD), WIDTH)
        middle, left, right = lanes_beside(surf[body_rows, pl.ds(c, WIDTH + 2 * PAD)], WIDTH)
        before = pltpu.roll(surf[pl.ds(0, rows + TILE), inner], 1, 0)[TILE:]
        after = pltpu.roll(surf[pl.ds(TILE, rows + TILE), inner], rows + TILE - 1, 0)[:rows]
        grad_rows = (after - before) * 0.5
        grad_cols = (right - left) * 0.5
        laplace = after + before + right + left - 4.0 * middle
        names = blocks[:, cols]
        rate = jnp.full(names.shape, rates[0], jnp.float32)
        for label in range(1, blocks_count):
            rate = jnp.where(names == label, rates[label], rate)
        tendency = -vel[0, :, cols] * grad_rows - vel[1, :, cols] * grad_cols + rate * laplace
        fresh = middle + TIME_STEP * flags[:, cols].astype(jnp.float32) * tendency
        moved[:, cols] = fresh
        shift[body_rows, cols] = fresh - middle
        return carry

    lax.fori_loop(0, steps, advect, 0)
    surface_out = pltpu.make_async_copy(moved, new_surface, out_sem.at[0])
    surface_out.start()
    locals_[4].wait()
    for side in (0, 1):
        pl.when(lat_sends[side])(shift_copies[side].start)
    for k in range(EARLY, CHUNKS):
        for side in (0, 1):
            pl.when(lat_sends[side])(first_copies[k][side].start)

    for side in (0, 1):
        pl.when(depth_recvs[side])(layer_copies[side].wait_recv)

    def profile_of(index):
        return (total_layers - index).astype(jnp.float32) / total_layers

    base = depth * layers
    profile = profile_of(base + lax.broadcasted_iota(jnp.int32, (layers, WIDTH), 0))
    above_profile = profile_of(base - 1)
    below_profile = profile_of(base + layers)

    def widen(r, c, top, bottom):
        cols = pl.ds(c, WIDTH)
        inner = pl.ds(pl.multiple_of(c + PAD, PAD), WIDTH)
        row_shift = shift[pl.ds(TILE - 1 + r, 1), cols]
        first[r, body_layers, inner] = (
            first[r, body_layers, inner] + jnp.broadcast_to(row_shift, (layers, WIDTH)) * profile
        )
        if top is not None:
            top(r, inner, row_shift)
            bottom(r, inner, row_shift)

    above = pl.ds(TILE - 1, 1)
    below = pl.ds(TILE + layers, 1)

    def own_rows(t, carry):
        r = t // steps + 1
        c = pl.multiple_of(lax.rem(t, steps) * WIDTH, WIDTH)

        def top(r, inner, row_shift):
            @pl.when(has_above)
            def _():
                first[r, above, inner] = first[r, above, inner] + row_shift * above_profile

            @pl.when(jnp.logical_not(has_above))
            def _():
                first[r, above, inner] = row_shift
                second[r, above, inner] = row_shift

        def bottom(r, inner, row_shift):
            @pl.when(has_below)
            def _():
                first[r, below, inner] = first[r, below, inner] + row_shift * below_profile

            @pl.when(jnp.logical_not(has_below))
            def _():
                first[r, below, inner] = jnp.zeros_like(row_shift)
                second[r, below, inner] = jnp.zeros_like(row_shift)

        widen(r, c, top, bottom)
        return carry

    lax.fori_loop(0, rows * steps, own_rows, 0)

    def relaxed(source, r, c):
        inner = pl.ds(pl.multiple_of(c + PAD, PAD), WIDTH)
        middle, left, right = lanes_beside(
            source[r, body_layers, pl.ds(c, WIDTH + 2 * PAD)], WIDTH
        )
        upper = pltpu.roll(source[r, pl.ds(0, layers + TILE), inner], 1, 0)[TILE:]
        lower = pltpu.roll(source[r, pl.ds(TILE, layers + TILE), inner], layers + TILE - 1, 0)[
            :layers
        ]
        across = source[r - 1, body_layers, inner] + source[r + 1, body_layers, inner]
        neighbours = across + (left + right) + (upper + lower)
        return (1.0 - RELAX_WEIGHT) * middle + (RELAX_WEIGHT / 6.0) * neighbours

    def sweep_once(r, c):
        inner = pl.ds(pl.multiple_of(c + PAD, PAD), WIDTH)
        second[r, body_layers, inner] = relaxed(first, r, c)

    def sweep_twice(r, c):
        value = relaxed(second, r, c)
        result[r - 1, :, pl.ds(c, WIDTH)] = value
        power = value * value
        part = jnp.zeros((TILE, PAD), jnp.float32)
        for top in range(0, layers, TILE):
            for start in range(0, WIDTH, PAD):
                part = part + power[top : top + TILE, start : start + PAD]
        squares[r - 1] = squares[r - 1] + part

    def over(low, count, visit):
        def body(t, carry):
            c = pl.multiple_of(lax.rem(t, steps) * WIDTH, WIDTH)
            visit(t // steps + low, c)
            return carry

        lax.fori_loop(0, count * steps, body, 0)

    over(2, rows - 2, sweep_once)
    for side in (0, 1):
        pl.when(depth_sends[side])(later_layers[0][side].start)

    per_piece = piece // WIDTH
    for side in (0, 1):
        pl.when(lat_recvs[side])(shift_copies[side].wait_recv)
    for k in range(CHUNKS):
        for side in (0, 1):

            @pl.when(lat_recvs[side])
            def _(side=side, k=k):
                first_copies[k][side].wait_recv()
                for j in range(per_piece):
                    widen(far_edge[side], k * piece + j * WIDTH, None, None)

            near = own_edge[1 - side]
            for j in range(per_piece):
                sweep_once(near, k * piece + j * WIDTH)
            pl.when(lat_sends[1 - side])(second_copies[k][1 - side].start)
    for j in (1, 2):
        for side in (0, 1):
            pl.when(depth_sends[side])(later_layers[j][side].start)

    for side in (0, 1):
        pl.when(depth_recvs[side])(later_layers[0][side].wait_recv)
    over(3, rows - 4, sweep_twice)
    over(2, 1, sweep_twice)
    over(rows - 1, 1, sweep_twice)
    inside = pltpu.make_async_copy(
        result.at[pl.ds(1, rows - 2)], field.at[pl.ds(1, rows - 2)], out_sem.at[1]
    )
    inside.start()
    for j in (1, 2):
        for side in (0, 1):
            pl.when(depth_recvs[side])(later_layers[j][side].wait_recv)
    outs = []
    for k in range(CHUNKS):
        for side in (0, 1):
            pl.when(lat_recvs[side])(second_copies[k][side].wait_recv)
            near = own_edge[1 - side]
            for j in range(per_piece):
                sweep_twice(near, k * piece + j * WIDTH)
            cols = pl.ds(k * piece, piece)
            out = pltpu.make_async_copy(
                result.at[near - 1, :, cols],
                field.at[near - 1, :, cols],
                out_sem.at[2 + 2 * k + side],
            )
            out.start()
            outs.append(out)

    sums[...] = jnp.sum(squares[...], axis=1)
    for copy in sum_copies:
        copy.start()
    surface_out.wait()
    inside.wait()
    for side in (0, 1):
        for copy in [surf_copies[side], shift_copies[side]] + [
            group[k][side] for group in (first_copies, second_copies) for k in range(CHUNKS)
        ]:
            pl.when(lat_sends[side])(copy.wait_send)
        for copy in [layer_copies[side]] + [later_layers[j][side] for j in range(3)]:
            pl.when(depth_sends[side])(copy.wait_send)
    total = sums[...]
    for k, copy in enumerate(sum_copies):
        copy.wait_recv()
        total = total + others[k]
    column = jnp.sum(total, axis=1, keepdims=True)
    square = jnp.broadcast_to(column, (rows, norm.shape[1]))
    ids = lax.broadcasted_iota(jnp.int32, square.shape, 0)
    lanes = lax.broadcasted_iota(jnp.int32, square.shape, 1)
    flat = jnp.sum(jnp.where(ids == lanes, square, 0.0), axis=0, keepdims=True)
    norm[...] = jnp.broadcast_to(jnp.sqrt(flat / (total_layers * columns)), norm.shape)
    for copy in sum_copies:
        copy.wait_send()
    for out in outs:
        out.wait()


def solution(mesh):
    lats, depths = mesh.shape["lat"], mesh.shape["depth"]

    def per_device(surface, velocity, block_map, free_flags, block_rates, previous_mesh):
        rows, layers, columns = previous_mesh.shape
        wide = columns + 2 * PAD
        anywhere = pl.BlockSpec(memory_space=pltpu.HBM)
        f32 = jnp.float32
        slots = 2 + 2 * CHUNKS
        others = max(depths - 1, 1)
        new_surface, field, norm = pl.pallas_call(
            functools.partial(kernel, lats, depths),
            out_shape=(
                jax.ShapeDtypeStruct(surface.shape, f32),
                jax.ShapeDtypeStruct(previous_mesh.shape, f32),
                jax.ShapeDtypeStruct((TILE, pl.cdiv(rows, PAD) * PAD), f32),
            ),
            in_specs=[anywhere] * 4 + [pl.BlockSpec(memory_space=pltpu.SMEM), anywhere],
            out_specs=(anywhere, anywhere, pl.BlockSpec(memory_space=pltpu.VMEM)),
            scratch_shapes=[
                pltpu.VMEM((rows + 2 * TILE, wide), f32),
                pltpu.VMEM(velocity.shape, f32),
                pltpu.VMEM(block_map.shape, jnp.int32),
                pltpu.VMEM(free_flags.shape, jnp.int32),
                pltpu.VMEM((rows + 2 * TILE, columns), f32),
                pltpu.VMEM(surface.shape, f32),
                pltpu.VMEM((rows + 2, layers + 2 * TILE, wide), f32),
                pltpu.VMEM((rows + 2, layers + 2 * TILE, wide), f32),
                pltpu.VMEM(previous_mesh.shape, f32),
                pltpu.VMEM((rows, TILE, PAD), f32),
                pltpu.VMEM((rows, PAD), f32),
                pltpu.VMEM((others, rows, PAD), f32),
                pltpu.SemaphoreType.DMA((5,)),
                pltpu.SemaphoreType.DMA((2 + 2 * CHUNKS,)),
                pltpu.SemaphoreType.DMA((2, slots)),
                pltpu.SemaphoreType.DMA((2, slots)),
                pltpu.SemaphoreType.DMA((2, 4)),
                pltpu.SemaphoreType.DMA((2, 4)),
                pltpu.SemaphoreType.DMA((others,)),
                pltpu.SemaphoreType.DMA((others,)),
            ],
            compiler_params=pltpu.CompilerParams(
                collective_id=0, has_side_effects=True, vmem_limit_bytes=62 * 1024 * 1024
            ),
            name="advect_and_relax",
        )(surface, velocity, block_map, free_flags, block_rates, previous_mesh)
        return new_surface, field, norm[0, :rows]

    return jax.shard_map(
        per_device,
        mesh=mesh,
        in_specs=(
            P("lat", None),
            P(None, "lat", None),
            P("lat", None),
            P("lat", None),
            P(),
            P("lat", "depth", None),
        ),
        out_specs=(P("lat", None), P("lat", "depth", None), P("lat")),
        check_vma=False,
    )
```

time: 112 us -> 56.6 us (0.51)
  the two profiles are of different devices: /device:TPU:11 before, /device:TPU:9 now
where the time goes in v1:
time: 56.6 us; the launch traced here: 56.4 us
  Pallas kernels  48.2 us (85%)
  local copies, waits for them, and re-layouts  7.51 us (13%)
  between operations  0.64 us (1%)
    pallas_call x1, Pallas kernels, per_device(): pl.pallas_call(functools.partial(kernel, lats, depths), out_shape=(jax.Sh...  48.2 us
    unnamed x2, local copies, waits for them, and re-layouts  6.32 us
    squeeze x1, local copies, waits for them, and re-layouts, per_device(): return (new_surface, field, norm[0, :rows])  1.19 us

profile of v1, /device:TPU:9, one launch (start us, length us, event | category | flops | bytes accessed | tf_op | source)
XLA Modules:
  0.0 56.4 jit_solution(8655444054479718961)
XLA Ops:
  0.6 48.2 %advect_and_relax.1 = (f32[16,4096]{1,0:T(8,128)}, f32[16,16,4096]{2,1,0:T(8,128)}, f32[8,128]{1,0:T(8,128)}) custom-call(f32[16,4096]{1,0:T(8,128)} %surface.1, f32[2,16,4096]{2,1,0:T(8,128)} %velocity.1, s32[16,4096]{1,0:T(8,128)} %block_map.1, s32[16,4096]{1,0:T(8,128)} %free_flags.1, f32[16]{0:T(128)} %rates.1, f32[16,16,4096]{2,1,0:T(8,128)} %previous.1), custom_call_target="tpu_custom_call" | custom-call | tf_op jit(solution)/shard_map/advect_and_relax/pallas_call | solution.py:462
  48.9 1.2 %slice_bitcast_fusion = f32[16]{0:T(128)} fusion(f32[8,128]{1,0:T(8,128)} %get-tuple-element.8), kind=kLoop, calls=%fused_computation | loop fusion | bytes 128 | tf_op jit(solution)/shard_map/squeeze | solution.py:498
  50.1 1.7 %copy.11 = f32[16,4096]{1,0:T(8,128)} copy(f32[16,4096]{1,0:T(8,128)} %get-tuple-element.12) | data formatting | bytes 524288
  51.7 4.7 %copy.12 = f32[16,16,4096]{2,1,0:T(8,128)} copy(f32[16,16,4096]{2,1,0:T(8,128)} %get-tuple-element.13) | data formatting | bytes 8388608

commit v2 on v1

--- a/solution.py
+++ b/solution.py
@@ -287,88 +287,62 @@
         return (total_layers - index).astype(jnp.float32) / total_layers
 
     base = depth * layers
-    profile = profile_of(base + lax.broadcasted_iota(jnp.int32, (layers, WIDTH), 0))
+    profile = profile_of(base + lax.broadcasted_iota(jnp.int32, (layers, PAD), 0))
     above_profile = profile_of(base - 1)
     below_profile = profile_of(base + layers)
-
-    def widen(r, c, top, bottom):
-        cols = pl.ds(c, WIDTH)
-        inner = pl.ds(pl.multiple_of(c + PAD, PAD), WIDTH)
-        row_shift = shift[pl.ds(TILE - 1 + r, 1), cols]
-        first[r, body_layers, inner] = (
-            first[r, body_layers, inner] + jnp.broadcast_to(row_shift, (layers, WIDTH)) * profile
-        )
-        if top is not None:
-            top(r, inner, row_shift)
-            bottom(r, inner, row_shift)
-
+    sublane = lax.broadcasted_iota(jnp.int32, (layers, WIDTH), 0)
+    at_first = sublane == 0
+    at_last = sublane == layers - 1
     above = pl.ds(TILE - 1, 1)
     below = pl.ds(TILE + layers, 1)
 
-    def own_rows(t, carry):
-        r = t // steps + 1
-        c = pl.multiple_of(lax.rem(t, steps) * WIDTH, WIDTH)
-
-        def top(r, inner, row_shift):
-            @pl.when(has_above)
-            def _():
-                first[r, above, inner] = first[r, above, inner] + row_shift * above_profile
-
-            @pl.when(jnp.logical_not(has_above))
-            def _():
-                first[r, above, inner] = row_shift
-                second[r, above, inner] = row_shift
-
-        def bottom(r, inner, row_shift):
-            @pl.when(has_below)
-            def _():
-                first[r, below, inner] = first[r, below, inner] + row_shift * below_profile
-
-            @pl.when(jnp.logical_not(has_below))
-            def _():
-                first[r, below, inner] = jnp.zeros_like(row_shift)
-                second[r, below, inner] = jnp.zeros_like(row_shift)
-
-        widen(r, c, top, bottom)
-        return carry
-
-    lax.fori_loop(0, rows * steps, own_rows, 0)
-
-    def relaxed(source, r, c):
-        inner = pl.ds(pl.multiple_of(c + PAD, PAD), WIDTH)
+    def widen(r, c):
+        inner = pl.ds(c + PAD, WIDTH)
+        row_shift = jnp.broadcast_to(shift[pl.ds(TILE - 1 + r, 1), pl.ds(c, WIDTH)], (layers, WIDTH))
+        wide_profile = jnp.concatenate([profile] * (WIDTH // PAD), axis=1)
+        first[r, body_layers, inner] = first[r, body_layers, inner] + row_shift * wide_profile
+
+    def relaxed(source, r, c, top, bottom):
+        inner = pl.ds(c + PAD, WIDTH)
         middle, left, right = lanes_beside(
             source[r, body_layers, pl.ds(c, WIDTH + 2 * PAD)], WIDTH
         )
-        upper = pltpu.roll(source[r, pl.ds(0, layers + TILE), inner], 1, 0)[TILE:]
-        lower = pltpu.roll(source[r, pl.ds(TILE, layers + TILE), inner], layers + TILE - 1, 0)[
-            :layers
-        ]
+        upper = jnp.where(at_first, top, pltpu.roll(middle, 1, 0))
+        lower = jnp.where(at_last, bottom, pltpu.roll(middle, layers - 1, 0))
         across = source[r - 1, body_layers, inner] + source[r + 1, body_layers, inner]
         neighbours = across + (left + right) + (upper + lower)
         return (1.0 - RELAX_WEIGHT) * middle + (RELAX_WEIGHT / 6.0) * neighbours
 
     def sweep_once(r, c):
-        inner = pl.ds(pl.multiple_of(c + PAD, PAD), WIDTH)
-        second[r, body_layers, inner] = relaxed(first, r, c)
+        inner = pl.ds(c + PAD, WIDTH)
+        row_shift = shift[pl.ds(TILE - 1 + r, 1), pl.ds(c, WIDTH)]
+        top = jnp.where(has_above, first[r, above, inner] + row_shift * above_profile, row_shift)
+        bottom = jnp.where(has_below, first[r, below, inner] + row_shift * below_profile, 0.0)
+        second[r, body_layers, inner] = relaxed(first, r, c, top, bottom)
 
     def sweep_twice(r, c):
-        value = relaxed(second, r, c)
+        inner = pl.ds(c + PAD, WIDTH)
+        row_shift = shift[pl.ds(TILE - 1 + r, 1), pl.ds(c, WIDTH)]
+        top = jnp.where(has_above, second[r, above, inner], row_shift)
+        bottom = jnp.where(has_below, second[r, below, inner], 0.0)
+        value = relaxed(second, r, c, top, bottom)
         result[r - 1, :, pl.ds(c, WIDTH)] = value
         power = value * value
-        part = jnp.zeros((TILE, PAD), jnp.float32)
+        part = squares[r - 1]
         for top in range(0, layers, TILE):
             for start in range(0, WIDTH, PAD):
                 part = part + power[top : top + TILE, start : start + PAD]
-        squares[r - 1] = squares[r - 1] + part
+        squares[r - 1] = part
 
     def over(low, count, visit):
         def body(t, carry):
-            c = pl.multiple_of(lax.rem(t, steps) * WIDTH, WIDTH)
-            visit(t // steps + low, c)
+            for step in range(steps):
+                visit(t, step * WIDTH)
             return carry
 
-        lax.fori_loop(0, count * steps, body, 0)
-
+        lax.fori_loop(low, low + count, body, 0)
+
+    over(1, rows, widen)
     over(2, rows - 2, sweep_once)
     for side in (0, 1):
         pl.when(depth_sends[side])(later_layers[0][side].start)
@@ -383,7 +357,7 @@
             def _(side=side, k=k):
                 first_copies[k][side].wait_recv()
                 for j in range(per_piece):
-                    widen(far_edge[side], k * piece + j * WIDTH, None, None)
+                    widen(far_edge[side], k * piece + j * WIDTH)
 
             near = own_edge[1 - side]
             for j in range(per_piece):

time: 56.6 us -> 41.8 us (0.74)
  the two profiles are of different devices: /device:TPU:9 before, /device:TPU:11 now
where the time goes in v2:
time: 41.8 us; the launch traced here: 41.6 us
  Pallas kernels  33.4 us (80%)
  local copies, waits for them, and re-layouts  7.51 us (18%)
  between operations  0.64 us (2%)
    pallas_call x1, Pallas kernels, per_device(): pl.pallas_call(functools.partial(kernel, lats, depths), out_shape=(jax.Sh...  33.4 us
    unnamed x2, local copies, waits for them, and re-layouts  6.32 us
    squeeze x1, local copies, waits for them, and re-layouts, per_device(): return (new_surface, field, norm[0, :rows])  1.19 us

profile of v2, /device:TPU:11, one launch (start us, length us, event | category | flops | bytes accessed | tf_op | source)
XLA Modules:
  0.0 41.6 jit_solution(16227439945400855415)
XLA Ops:
  0.6 33.4 %advect_and_relax.1 = (f32[16,4096]{1,0:T(8,128)}, f32[16,16,4096]{2,1,0:T(8,128)}, f32[8,128]{1,0:T(8,128)}) custom-call(f32[16,4096]{1,0:T(8,128)} %surface.1, f32[2,16,4096]{2,1,0:T(8,128)} %velocity.1, s32[16,4096]{1,0:T(8,128)} %block_map.1, s32[16,4096]{1,0:T(8,128)} %free_flags.1, f32[16]{0:T(128)} %rates.1, f32[16,16,4096]{2,1,0:T(8,128)} %previous.1), custom_call_target="tpu_custom_call" | custom-call | tf_op jit(solution)/shard_map/advect_and_relax/pallas_call | solution.py:436
  34.1 1.2 %slice_bitcast_fusion = f32[16]{0:T(128)} fusion(f32[8,128]{1,0:T(8,128)} %get-tuple-element.8), kind=kLoop, calls=%fused_computation | loop fusion | bytes 128 | tf_op jit(solution)/shard_map/squeeze | solution.py:472
  35.3 1.7 %copy.11 = f32[16,4096]{1,0:T(8,128)} copy(f32[16,4096]{1,0:T(8,128)} %get-tuple-element.12) | data formatting | bytes 524288
  36.9 4.7 %copy.12 = f32[16,16,4096]{2,1,0:T(8,128)} copy(f32[16,16,4096]{2,1,0:T(8,128)} %get-tuple-element.13) | data formatting | bytes 8388608

commit v3 on v2

--- a/solution.py
+++ b/solution.py
@@ -43,15 +43,12 @@
     blocks,
     flags,
     shift,
-    moved,
     first,
     second,
-    result,
     squares,
     sums,
     others,
     local_sem,
-    out_sem,
     lat_send,
     lat_recv,
     depth_send,
@@ -266,13 +263,11 @@
             rate = jnp.where(names == label, rates[label], rate)
         tendency = -vel[0, :, cols] * grad_rows - vel[1, :, cols] * grad_cols + rate * laplace
         fresh = middle + TIME_STEP * flags[:, cols].astype(jnp.float32) * tendency
-        moved[:, cols] = fresh
+        new_surface[:, cols] = fresh
         shift[body_rows, cols] = fresh - middle
         return carry
 
     lax.fori_loop(0, steps, advect, 0)
-    surface_out = pltpu.make_async_copy(moved, new_surface, out_sem.at[0])
-    surface_out.start()
     locals_[4].wait()
     for side in (0, 1):
         pl.when(lat_sends[side])(shift_copies[side].start)
@@ -326,7 +321,7 @@
         top = jnp.where(has_above, second[r, above, inner], row_shift)
         bottom = jnp.where(has_below, second[r, below, inner], 0.0)
         value = relaxed(second, r, c, top, bottom)
-        result[r - 1, :, pl.ds(c, WIDTH)] = value
+        field[r - 1, :, pl.ds(c, WIDTH)] = value
         power = value * value
         part = squares[r - 1]
         for top in range(0, layers, TILE):
@@ -372,34 +367,19 @@
     over(3, rows - 4, sweep_twice)
     over(2, 1, sweep_twice)
     over(rows - 1, 1, sweep_twice)
-    inside = pltpu.make_async_copy(
-        result.at[pl.ds(1, rows - 2)], field.at[pl.ds(1, rows - 2)], out_sem.at[1]
-    )
-    inside.start()
     for j in (1, 2):
         for side in (0, 1):
             pl.when(depth_recvs[side])(later_layers[j][side].wait_recv)
-    outs = []
     for k in range(CHUNKS):
         for side in (0, 1):
             pl.when(lat_recvs[side])(second_copies[k][side].wait_recv)
             near = own_edge[1 - side]
             for j in range(per_piece):
                 sweep_twice(near, k * piece + j * WIDTH)
-            cols = pl.ds(k * piece, piece)
-            out = pltpu.make_async_copy(
-                result.at[near - 1, :, cols],
-                field.at[near - 1, :, cols],
-                out_sem.at[2 + 2 * k + side],
-            )
-            out.start()
-            outs.append(out)
 
     sums[...] = jnp.sum(squares[...], axis=1)
     for copy in sum_copies:
         copy.start()
-    surface_out.wait()
-    inside.wait()
     for side in (0, 1):
         for copy in [surf_copies[side], shift_copies[side]] + [
             group[k][side] for group in (first_copies, second_copies) for k in range(CHUNKS)
@@ -419,8 +399,6 @@
     norm[...] = jnp.broadcast_to(jnp.sqrt(flat / (total_layers * columns)), norm.shape)
     for copy in sum_copies:
         copy.wait_send()
-    for out in outs:
-        out.wait()
 
 
 def solution(mesh):
@@ -433,30 +411,31 @@
         f32 = jnp.float32
         slots = 2 + 2 * CHUNKS
         others = max(depths - 1, 1)
+        held = [
+            pltpu.with_memory_space_constraint(value, pltpu.HBM)
+            for value in (surface, velocity, block_map, free_flags, previous_mesh)
+        ]
         new_surface, field, norm = pl.pallas_call(
             functools.partial(kernel, lats, depths),
             out_shape=(
-                jax.ShapeDtypeStruct(surface.shape, f32),
-                jax.ShapeDtypeStruct(previous_mesh.shape, f32),
-                jax.ShapeDtypeStruct((TILE, pl.cdiv(rows, PAD) * PAD), f32),
+                pltpu.VMEM(surface.shape, f32),
+                pltpu.VMEM(previous_mesh.shape, f32),
+                pltpu.VMEM((TILE, pl.cdiv(rows, PAD) * PAD), f32),
             ),
             in_specs=[anywhere] * 4 + [pl.BlockSpec(memory_space=pltpu.SMEM), anywhere],
-            out_specs=(anywhere, anywhere, pl.BlockSpec(memory_space=pltpu.VMEM)),
+            out_specs=(pl.BlockSpec(memory_space=pltpu.VMEM),) * 3,
             scratch_shapes=[
                 pltpu.VMEM((rows + 2 * TILE, wide), f32),
                 pltpu.VMEM(velocity.shape, f32),
                 pltpu.VMEM(block_map.shape, jnp.int32),
                 pltpu.VMEM(free_flags.shape, jnp.int32),
                 pltpu.VMEM((rows + 2 * TILE, columns), f32),
-                pltpu.VMEM(surface.shape, f32),
                 pltpu.VMEM((rows + 2, layers + 2 * TILE, wide), f32),
                 pltpu.VMEM((rows + 2, layers + 2 * TILE, wide), f32),
-                pltpu.VMEM(previous_mesh.shape, f32),
                 pltpu.VMEM((rows, TILE, PAD), f32),
                 pltpu.VMEM((rows, PAD), f32),
                 pltpu.VMEM((others, rows, PAD), f32),
                 pltpu.SemaphoreType.DMA((5,)),
-                pltpu.SemaphoreType.DMA((2 + 2 * CHUNKS,)),
                 pltpu.SemaphoreType.DMA((2, slots)),
                 pltpu.SemaphoreType.DMA((2, slots)),
                 pltpu.SemaphoreType.DMA((2, 4)),
@@ -465,10 +444,10 @@
                 pltpu.SemaphoreType.DMA((others,)),
             ],
             compiler_params=pltpu.CompilerParams(
-                collective_id=0, has_side_effects=True, vmem_limit_bytes=62 * 1024 * 1024
+                collective_id=0, has_side_effects=True, vmem_limit_bytes=56 * 1024 * 1024
             ),
             name="advect_and_relax",
-        )(surface, velocity, block_map, free_flags, block_rates, previous_mesh)
+        )(*held[:4], block_rates, held[4])
         return new_surface, field, norm[0, :rows]
 
     return jax.shard_map(

time: 41.8 us -> 36.8 us (0.88)
  local copies, waits for them, and re-layouts: 7.51 us -> 3.23 us
  Pallas kernels: 33.4 us -> 32.7 us
    unnamed x2, local copies, waits for them, and re-layouts: 6.32 us -> 2.72 us
    pallas_call x1, Pallas kernels: 33.4 us -> 32.7 us  [per_device(): pl.pallas_call(functools.partial(kernel, lats, depths), out_shape=(pltpu....]
    squeeze x1, local copies, waits for them, and re-layouts: 1.19 us -> 0.51 us  [per_device(): return (new_surface, field, norm[0, :rows])]
where the time goes in v3:
time: 36.8 us; the launch traced here: 36.6 us
  Pallas kernels  32.7 us (89%)
  local copies, waits for them, and re-layouts  3.23 us (9%)
  between operations  0.64 us (2%)
    pallas_call x1, Pallas kernels, per_device(): pl.pallas_call(functools.partial(kernel, lats, depths), out_shape=(pltpu....  32.7 us
    unnamed x2, local copies, waits for them, and re-layouts  2.72 us

profile of v3, /device:TPU:11, one launch (start us, length us, event | category | flops | bytes accessed | tf_op | source)
XLA Modules:
  0.0 36.6 jit_solution(17465187670093155766)
XLA Ops:
  0.6 32.7 %advect_and_relax.1 = (f32[16,4096]{1,0:T(8,128)S(1)}, f32[16,16,4096]{2,1,0:T(8,128)S(1)}, f32[8,128]{1,0:T(8,128)S(1)}) custom-call(f32[16,4096]{1,0:T(8,128)} %surface.1, f32[2,16,4096]{2,1,0:T(8,128)} %velocity.1, s32[16,4096]{1,0:T(8,128)} %block_map.1, s32[16,4096]{1,0:T(8,128)} %free_flags.1, f32[16]{0:T(128)} %rates.1, f32[16,16,4096]{2,1,0:T(8,128)} %previous.1), custom_call_target="tpu_custom_call" | custom-call | tf_op jit(solution)/shard_map/advect_and_relax/pallas_call | solution.py:418
  33.4 0.7 %copy.11 = f32[16,4096]{1,0:T(8,128)} copy(f32[16,4096]{1,0:T(8,128)S(1)} %get-tuple-element.9) | data formatting | bytes 524288
  34.1 0.5 %slice_bitcast_fusion = f32[16]{0:T(128)} fusion(f32[8,128]{1,0:T(8,128)S(1)} %get-tuple-element.8), kind=kLoop, calls=%fused_computation | loop fusion | bytes 128 | tf_op jit(solution)/shard_map/squeeze | solution.py:451
  34.6 2.0 %copy.12 = f32[16,16,4096]{2,1,0:T(8,128)} copy(f32[16,16,4096]{2,1,0:T(8,128)S(1)} %get-tuple-element.10) | data formatting | bytes 8388608

commit v4 on v3

--- a/solution.py
+++ b/solution.py
@@ -134,7 +134,7 @@
         lateral(
             side,
             SURF,
-            surface.at[pl.ds((rows - 1, 0)[side], 1), :],
+            surf.at[pl.ds((TILE + rows - 1, TILE)[side], 1), body_cols],
             surf.at[pl.ds((TILE - 1, TILE + rows)[side], 1), body_cols],
         )
         for side in (0, 1)
@@ -206,6 +206,7 @@
         for k in range(1, depths)
     ]
 
+    locals_[0].wait()
     for side in (0, 1):
         pl.when(lat_sends[side])(surf_copies[side].start)
     for side in (0, 1):
@@ -242,7 +243,7 @@
                     (layers, columns), jnp.float32
                 )
 
-    for copy in locals_[:4]:
+    for copy in locals_[1:4]:
         copy.wait()
     for side in (0, 1):
         pl.when(lat_recvs[side])(surf_copies[side].wait_recv)

time: 36.8 us -> 36.6 us (level)
  no operation moved by 1% of the time
where the time goes in v4:
time: 36.6 us; the launch traced here: 36.4 us
  Pallas kernels  32.5 us (89%)
  local copies, waits for them, and re-layouts  3.23 us (9%)
  between operations  0.64 us (2%)
    pallas_call x1, Pallas kernels, per_device(): pl.pallas_call(functools.partial(kernel, lats, depths), out_shape=(pltpu....  32.5 us
    unnamed x2, local copies, waits for them, and re-layouts  2.72 us

profile of v4, /device:TPU:11, one launch (start us, length us, event | category | flops | bytes accessed | tf_op | source)
XLA Modules:
  0.0 36.4 jit_solution(11024866910018130369)
XLA Ops:
  0.6 32.5 %advect_and_relax.1 = (f32[16,4096]{1,0:T(8,128)S(1)}, f32[16,16,4096]{2,1,0:T(8,128)S(1)}, f32[8,128]{1,0:T(8,128)S(1)}) custom-call(f32[16,4096]{1,0:T(8,128)} %surface.1, f32[2,16,4096]{2,1,0:T(8,128)} %velocity.1, s32[16,4096]{1,0:T(8,128)} %block_map.1, s32[16,4096]{1,0:T(8,128)} %free_flags.1, f32[16]{0:T(128)} %rates.1, f32[16,16,4096]{2,1,0:T(8,128)} %previous.1), custom_call_target="tpu_custom_call" | custom-call | tf_op jit(solution)/shard_map/advect_and_relax/pallas_call | solution.py:419
  33.2 0.7 %copy.11 = f32[16,4096]{1,0:T(8,128)} copy(f32[16,4096]{1,0:T(8,128)S(1)} %get-tuple-element.9) | data formatting | bytes 524288
  33.9 0.5 %slice_bitcast_fusion = f32[16]{0:T(128)} fusion(f32[8,128]{1,0:T(8,128)S(1)} %get-tuple-element.8), kind=kLoop, calls=%fused_computation | loop fusion | bytes 128 | tf_op jit(solution)/shard_map/squeeze | solution.py:452
  34.4 2.0 %copy.12 = f32[16,16,4096]{2,1,0:T(8,128)} copy(f32[16,16,4096]{2,1,0:T(8,128)S(1)} %get-tuple-element.10) | data formatting | bytes 8388608
